TPU v7x, 32 devices: a whole 2x2x4 slice. The times are simulated.
32 devices in a mesh: section: 4 (over x, core), row: 2 (over y), col: 4 (over z).
Axes of the slice: x: 2, y: 2, z: 4, core: 2. Of those that a mesh axis runs over, the one named last changes fastest.
Arguments:
- hidden: bfloat16 [4, 8, 4096], P(None, None, 'col'), may hold values from -6 to 6
- norm_gain: bfloat16 [4, 4096], P('section', 'col'), may hold values from 0.25 to 1.75
- w_qkv: bfloat16 [4, 4096, 6144], P('section', 'col', 'row'), may hold values from -0.09375 to 0.09375
- w_out: bfloat16 [4, 4096, 4096], P('section', 'row', 'col'), may hold values from -0.09375 to 0.09375
- cache_keys: bfloat16 [4, 4, 8, 128, 8, 128], P('section', None, 'col', None, 'row'), may hold values from -240 to 240, as said below
- cache_values: bfloat16 [4, 4, 8, 128, 8, 128], P('section', None, 'col', None, 'row'), may hold values from -6 to 6
- cache_lengths: int32 [4, 8], P(None, 'col'), may hold values from 1 to 127
Outputs:
- layer_outputs: bfloat16 [4, 4, 8, 4096], P('section', None, None, 'col')
Inputs may be any that keep to these rules, and one draw needn't show every extreme that they name: `cache_keys`: cached keys are of order one except that some sequences may carry much larger keys at a few positions.
All inputs are finite; a program needn't handle non-finite values.
Results may differ from a plain program's by a relative error of at most 0.04.
Values may be sent and summed in bfloat16 or wider, within the bound.
A program may use at most 64 MiB of HBM per device.

v0:
```python
import jax
import jax.numpy as jnp
from jax import lax
from jax.sharding import PartitionSpec as P

D = 4096
HEADS = 32
KVH = 8


def from_behind(x, axis, by):
    peers = lax.axis_size(axis)
    pairs = [(i, i + by) for i in range(peers) if 0 <= i + by < peers]
    return lax.ppermute(x, axis, pairs)


def rotate(vectors, positions):
    half_dim = vectors.shape[-1] // 2
    inverse_freq = 500000.0 ** (-jnp.arange(half_dim, dtype=jnp.float32) * 2.0 / vectors.shape[-1])
    angles = positions * inverse_freq
    angles = jnp.concatenate([angles, angles], axis=-1)
    swapped = jnp.concatenate([-vectors[..., half_dim:], vectors[..., :half_dim]], axis=-1)
    return vectors * jnp.cos(angles) + swapped * jnp.sin(angles)


def attend(queries, new_key, new_value, key_block, value_block, length):
    score_scale = 1.0 / jnp.sqrt(jnp.float32(queries.shape[-1]))
    scores = (
        jnp.einsum("bgrd,bjgd->bgrj", queries, key_block, preferred_element_type=jnp.float32)
        * score_scale
    )
    own_score = (
        jnp.einsum("bgrd,bgd->bgr", queries, new_key, preferred_element_type=jnp.float32)
        * score_scale
    )
    visible = jnp.arange(key_block.shape[1])[None, :] < length[:, None]
    scores = jnp.where(visible[:, None, None, :], scores, -jnp.inf)
    row_max = jnp.maximum(jnp.max(scores, axis=-1), own_score)
    cache_exp = jnp.exp(scores - row_max[..., None])
    own_exp = jnp.exp(own_score - row_max)
    total = jnp.sum(cache_exp, axis=-1) + own_exp
    cache_weight = (cache_exp / total[..., None]).astype(jnp.bfloat16)
    own_weight = (own_exp / total).astype(jnp.bfloat16)
    result = jnp.einsum(
        "bgrj,bjgd->bgrd", cache_weight, value_block, preferred_element_type=jnp.float32
    )
    result = (
        result
        + own_weight.astype(jnp.float32)[..., None] * new_value.astype(jnp.float32)[:, :, None, :]
    )
    return result.astype(jnp.bfloat16)


def shards(hidden, norm_gain, w_qkv, w_out, cache_keys, cache_values, cache_lengths):
    section_count = lax.axis_size("section")
    section_at = lax.axis_index("section")
    col_count = lax.axis_size("col")
    micro_count = hidden.shape[0]
    batch_size = hidden.shape[1]
    seq_part = batch_size // col_count
    gain_row = norm_gain[0]
    proj_weight = w_qkv[0]
    out_weight = w_out[0]
    groups = cache_keys.shape[4]
    head_dim = cache_keys.shape[5]
    per_group = HEADS // KVH
    tick_count = micro_count + section_count - 1

    def layer_part(current, key_block, value_block, length):
        h_float = current.astype(jnp.float32)
        scaled = (h_float * gain_row.astype(jnp.float32)).astype(jnp.bfloat16)
        squares = jnp.sum(h_float * h_float, axis=1)
        partial_value = jnp.dot(scaled, proj_weight, preferred_element_type=jnp.float32)
        projected, own_squares = (
            lax.psum_scatter(partial_value, "col", scatter_dimension=0, tiled=True),
            lax.psum_scatter(squares, "col", scatter_dimension=0, tiled=True),
        )
        factor = lax.rsqrt(own_squares / D + 1e-05)
        projected = (projected * factor[:, None]).reshape(seq_part, groups, per_group + 2, head_dim)
        positions = length.astype(jnp.float32)
        queries = rotate(projected[:, :, :per_group], positions[:, None, None, None]).astype(
            jnp.bfloat16
        )
        new_key = rotate(projected[:, :, per_group], positions[:, None, None]).astype(jnp.bfloat16)
        new_value = projected[:, :, per_group + 1].astype(jnp.bfloat16)
        attended = attend(queries, new_key, new_value, key_block, value_block, length)
        attended = attended.reshape(seq_part, groups * per_group * head_dim)
        mixed_rows = jnp.dot(
            lax.all_gather(attended, "col", axis=0, tiled=True),
            out_weight,
            preferred_element_type=jnp.float32,
        )
        summed = lax.psum(mixed_rows, "row")
        return (h_float + summed).astype(jnp.bfloat16)

    def advance(tick_at, loop_state):
        received, collected = loop_state
        micro_at = tick_at - section_at
        active = (micro_at >= 0) & (micro_at < micro_count)
        micro_pick = jnp.clip(micro_at, 0, micro_count - 1)
        entry_rows = lax.dynamic_index_in_dim(
            hidden, jnp.clip(tick_at, 0, micro_count - 1), 0, keepdims=False
        )
        current = jnp.where(section_at == 0, entry_rows, received)
        key_block = lax.dynamic_index_in_dim(cache_keys[0], micro_pick, 0, keepdims=False)
        value_block = lax.dynamic_index_in_dim(cache_values[0], micro_pick, 0, keepdims=False)
        length = lax.dynamic_index_in_dim(cache_lengths, micro_pick, 0, keepdims=False)
        produced = layer_part(current, key_block, value_block, length)
        previous = lax.dynamic_index_in_dim(collected, micro_pick, 0, keepdims=False)
        stored = jnp.where(active, produced, previous)
        collected = lax.dynamic_update_index_in_dim(collected, stored, micro_pick, 0)
        received = from_behind(produced, "section", 1)
        return (received, collected)

    start_rows = jnp.zeros(hidden.shape[1:], jnp.bfloat16)
    start_collected = jnp.zeros(hidden.shape, jnp.bfloat16)
    received, collected = lax.fori_loop(0, tick_count, advance, (start_rows, start_collected))
    return collected[None]


def solution(mesh):
    return jax.shard_map(
        shards,
        mesh=mesh,
        in_specs=(
            P(None, None, "col"),
            P("section", "col"),
            P("section", "col", "row"),
            P("section", "row", "col"),
            P("section", None, "col", None, "row", None),
            P("section", None, "col", None, "row", None),
            P(None, "col"),
        ),
        out_specs=P("section", None, None, "col"),
        check_vma=False,
    )
```

profile of v0, /device:TPU:1, one launch (start us, length us, event | category | flops | bytes accessed | tf_op | source)
XLA Modules:
  0.0 510.5 jit_solution(13046033242243475409)
XLA Ops:
  8.0 495.0 %while.18 = (s32[]{:T(128)}, bf16[8,1024]{1,0:T(8,128)(2,1)S(1)}, bf16[4,8,1024]{2,1,0:T(8,128)(2,1)S(1)}, pred[]{:T(512)}, bf16[4,8,1024]{2,1,0:T(8,128)(2,1)},...) while((s32[]{:T(128)}, bf16[8,1024]{1,0:T(8,128)(2,1)S(1)}, ...), condition=%wide.region_7.8_spmd, body=%wide.region_0.7_spmd.sunk | while | flops 86196720 | bytes 13568984 | solution.py:117
  9.0 4.3 fusion.65
  13.7 10.8 %all-reduce.5 = f32[8]{0:T(128)S(1)} all-reduce(f32[8]{0:T(128)S(1)} %get-tuple-element.477), channel_id=3, replica_groups=mesh['section'=4,'row'=2,'col'=4] {'col'}, use_global_device_ids=true, to_apply=%region_3.3.clone | all-reduce | flops 8 | bytes 64 | tf_op jit(solution)/shard_map/while
  26.9 21.0 %all-reduce.8.cloned.1.call-done = f32[8,3072]{1,0:T(8,128)} async-done(((f32[8,3072]{1,0:T(8,128)}), f32[8,3072]{1,0:T(8,128)}) %all-reduce.8.cloned.1.call-update) | async-done | bytes 98320 | tf_op jit(solution)/shard_map/while
  50.2 10.3 %all-gather.2 = bf16[4,2,2048]{2,1,0:T(2,128)(2,1)S(1)} all-gather(bf16[1,2,2048]{2,1,0:T(2,128)(2,1)S(1)} %reshape.350), channel_id=1, replica_groups=mesh['section'=4,'row'=2,'col'=4] {'col'}, dimensions={0}, use_global_device_ids=true | all-gather | bytes 40960 | tf_op jit(solution)/shard_map/while/body/eval_jaxpr/all_gather | solution.py:89
  60.5 2.8 fusion.77
  63.3 6.3 %psum.16 = f32[8,1024]{1,0:T(8,128)S(1)} all-reduce(f32[8,1024]{1,0:T(8,128)S(1)} %fusion.77), channel_id=1, replica_groups=mesh['section'=4,'row'=2,'col'=4] {'row'}, use_global_device_ids=true, to_apply=%region_6.6 | all-reduce | flops 8192 | bytes 65536 | tf_op jit(solution)/shard_map/while/body/eval_jaxpr/psum | solution.py:93
  69.6 10.6 %collective-permute-start = (bf16[8,1024]{1,0:T(8,128)(2,1)S(1)}, bf16[8,1024]{1,0:T(8,128)(2,1)S(1)}, u32[]{:S(2)}, u32[]{:S(2)}) collective-permute-start(bf16[8,1024]{1,0:T(8,128)(2,1)S(1)} %get-tuple-element.491), channel_id=1, source_target_pairs={{0,8},{8,16},{16,24},{1,9},{9,17},{17,25},{2,10},{10,18},{18,26},{... | collective-permute-start | bytes 49160 | tf_op jit(solution)/shard_map/while/body/eval_jaxpr/ppermute | solution.py:14
  82.0 4.3 fusion.65
  86.7 8.6 %all-reduce.5 = f32[8]{0:T(128)S(1)} all-reduce(f32[8]{0:T(128)S(1)} %get-tuple-element.477), channel_id=3, replica_groups=mesh['section'=4,'row'=2,'col'=4] {'col'}, use_global_device_ids=true, to_apply=%region_3.3.clone | all-reduce | flops 8 | bytes 64 | tf_op jit(solution)/shard_map/while
  97.7 20.6 %all-reduce.8.cloned.1.call-done = f32[8,3072]{1,0:T(8,128)} async-done(((f32[8,3072]{1,0:T(8,128)}), f32[8,3072]{1,0:T(8,128)}) %all-reduce.8.cloned.1.call-update) | async-done | bytes 98320 | tf_op jit(solution)/shard_map/while
  120.5 10.3 %all-gather.2 = bf16[4,2,2048]{2,1,0:T(2,128)(2,1)S(1)} all-gather(bf16[1,2,2048]{2,1,0:T(2,128)(2,1)S(1)} %reshape.350), channel_id=1, replica_groups=mesh['section'=4,'row'=2,'col'=4] {'col'}, dimensions={0}, use_global_device_ids=true | all-gather | bytes 40960 | tf_op jit(solution)/shard_map/while/body/eval_jaxpr/all_gather | solution.py:89
  130.8 2.8 fusion.77
  133.6 6.3 %psum.16 = f32[8,1024]{1,0:T(8,128)S(1)} all-reduce(f32[8,1024]{1,0:T(8,128)S(1)} %fusion.77), channel_id=1, replica_groups=mesh['section'=4,'row'=2,'col'=4] {'row'}, use_global_device_ids=true, to_apply=%region_6.6 | all-reduce | flops 8192 | bytes 65536 | tf_op jit(solution)/shard_map/while/body/eval_jaxpr/psum | solution.py:93
  140.0 10.6 %collective-permute-start = (bf16[8,1024]{1,0:T(8,128)(2,1)S(1)}, bf16[8,1024]{1,0:T(8,128)(2,1)S(1)}, u32[]{:S(2)}, u32[]{:S(2)}) collective-permute-start(bf16[8,1024]{1,0:T(8,128)(2,1)S(1)} %get-tuple-element.491), channel_id=1, source_target_pairs={{0,8},{8,16},{16,24},{1,9},{9,17},{17,25},{2,10},{10,18},{18,26},{... | collective-permute-start | bytes 49160 | tf_op jit(solution)/shard_map/while/body/eval_jaxpr/ppermute | solution.py:14
  152.3 4.3 fusion.65
  157.0 8.6 %all-reduce.5 = f32[8]{0:T(128)S(1)} all-reduce(f32[8]{0:T(128)S(1)} %get-tuple-element.477), channel_id=3, replica_groups=mesh['section'=4,'row'=2,'col'=4] {'col'}, use_global_device_ids=true, to_apply=%region_3.3.clone | all-reduce | flops 8 | bytes 64 | tf_op jit(solution)/shard_map/while
  168.0 20.5 %all-reduce.8.cloned.1.call-done = f32[8,3072]{1,0:T(8,128)} async-done(((f32[8,3072]{1,0:T(8,128)}), f32[8,3072]{1,0:T(8,128)}) %all-reduce.8.cloned.1.call-update) | async-done | bytes 98320 | tf_op jit(solution)/shard_map/while
  190.8 10.3 %all-gather.2 = bf16[4,2,2048]{2,1,0:T(2,128)(2,1)S(1)} all-gather(bf16[1,2,2048]{2,1,0:T(2,128)(2,1)S(1)} %reshape.350), channel_id=1, replica_groups=mesh['section'=4,'row'=2,'col'=4] {'col'}, dimensions={0}, use_global_device_ids=true | all-gather | bytes 40960 | tf_op jit(solution)/shard_map/while/body/eval_jaxpr/all_gather | solution.py:89
  201.1 2.8 fusion.77
  204.0 6.3 %psum.16 = f32[8,1024]{1,0:T(8,128)S(1)} all-reduce(f32[8,1024]{1,0:T(8,128)S(1)} %fusion.77), channel_id=1, replica_groups=mesh['section'=4,'row'=2,'col'=4] {'row'}, use_global_device_ids=true, to_apply=%region_6.6 | all-reduce | flops 8192 | bytes 65536 | tf_op jit(solution)/shard_map/while/body/eval_jaxpr/psum | solution.py:93
  210.3 10.6 %collective-permute-start = (bf16[8,1024]{1,0:T(8,128)(2,1)S(1)}, bf16[8,1024]{1,0:T(8,128)(2,1)S(1)}, u32[]{:S(2)}, u32[]{:S(2)}) collective-permute-start(bf16[8,1024]{1,0:T(8,128)(2,1)S(1)} %get-tuple-element.491), channel_id=1, source_target_pairs={{0,8},{8,16},{16,24},{1,9},{9,17},{17,25},{2,10},{10,18},{18,26},{... | collective-permute-start | bytes 49160 | tf_op jit(solution)/shard_map/while/body/eval_jaxpr/ppermute | solution.py:14
  222.6 4.3 fusion.65
  227.3 8.6 %all-reduce.5 = f32[8]{0:T(128)S(1)} all-reduce(f32[8]{0:T(128)S(1)} %get-tuple-element.477), channel_id=3, replica_groups=mesh['section'=4,'row'=2,'col'=4] {'col'}, use_global_device_ids=true, to_apply=%region_3.3.clone | all-reduce | flops 8 | bytes 64 | tf_op jit(solution)/shard_map/while
  238.3 20.5 %all-reduce.8.cloned.1.call-done = f32[8,3072]{1,0:T(8,128)} async-done(((f32[8,3072]{1,0:T(8,128)}), f32[8,3072]{1,0:T(8,128)}) %all-reduce.8.cloned.1.call-update) | async-done | bytes 98320 | tf_op jit(solution)/shard_map/while
  261.2 10.3 %all-gather.2 = bf16[4,2,2048]{2,1,0:T(2,128)(2,1)S(1)} all-gather(bf16[1,2,2048]{2,1,0:T(2,128)(2,1)S(1)} %reshape.350), channel_id=1, replica_groups=mesh['section'=4,'row'=2,'col'=4] {'col'}, dimensions={0}, use_global_device_ids=true | all-gather | bytes 40960 | tf_op jit(solution)/shard_map/while/body/eval_jaxpr/all_gather | solution.py:89
  271.4 2.8 fusion.77
  274.3 6.3 %psum.16 = f32[8,1024]{1,0:T(8,128)S(1)} all-reduce(f32[8,1024]{1,0:T(8,128)S(1)} %fusion.77), channel_id=1, replica_groups=mesh['section'=4,'row'=2,'col'=4] {'row'}, use_global_device_ids=true, to_apply=%region_6.6 | all-reduce | flops 8192 | bytes 65536 | tf_op jit(solution)/shard_map/while/body/eval_jaxpr/psum | solution.py:93
  280.6 10.6 %collective-permute-start = (bf16[8,1024]{1,0:T(8,128)(2,1)S(1)}, bf16[8,1024]{1,0:T(8,128)(2,1)S(1)}, u32[]{:S(2)}, u32[]{:S(2)}) collective-permute-start(bf16[8,1024]{1,0:T(8,128)(2,1)S(1)} %get-tuple-element.491), channel_id=1, source_target_pairs={{0,8},{8,16},{16,24},{1,9},{9,17},{17,25},{2,10},{10,18},{18,26},{... | collective-permute-start | bytes 49160 | tf_op jit(solution)/shard_map/while/body/eval_jaxpr/ppermute | solution.py:14
  292.9 4.3 fusion.65
  297.6 8.6 %all-reduce.5 = f32[8]{0:T(128)S(1)} all-reduce(f32[8]{0:T(128)S(1)} %get-tuple-element.477), channel_id=3, replica_groups=mesh['section'=4,'row'=2,'col'=4] {'col'}, use_global_device_ids=true, to_apply=%region_3.3.clone | all-reduce | flops 8 | bytes 64 | tf_op jit(solution)/shard_map/while
  308.7 20.5 %all-reduce.8.cloned.1.call-done = f32[8,3072]{1,0:T(8,128)} async-done(((f32[8,3072]{1,0:T(8,128)}), f32[8,3072]{1,0:T(8,128)}) %all-reduce.8.cloned.1.call-update) | async-done | bytes 98320 | tf_op jit(solution)/shard_map/while
  331.5 10.3 %all-gather.2 = bf16[4,2,2048]{2,1,0:T(2,128)(2,1)S(1)} all-gather(bf16[1,2,2048]{2,1,0:T(2,128)(2,1)S(1)} %reshape.350), channel_id=1, replica_groups=mesh['section'=4,'row'=2,'col'=4] {'col'}, dimensions={0}, use_global_device_ids=true | all-gather | bytes 40960 | tf_op jit(solution)/shard_map/while/body/eval_jaxpr/all_gather | solution.py:89
  341.8 2.8 fusion.77
  344.6 6.3 %psum.16 = f32[8,1024]{1,0:T(8,128)S(1)} all-reduce(f32[8,1024]{1,0:T(8,128)S(1)} %fusion.77), channel_id=1, replica_groups=mesh['section'=4,'row'=2,'col'=4] {'row'}, use_global_device_ids=true, to_apply=%region_6.6 | all-reduce | flops 8192 | bytes 65536 | tf_op jit(solution)/shard_map/while/body/eval_jaxpr/psum | solution.py:93
  350.9 10.6 %collective-permute-start = (bf16[8,1024]{1,0:T(8,128)(2,1)S(1)}, bf16[8,1024]{1,0:T(8,128)(2,1)S(1)}, u32[]{:S(2)}, u32[]{:S(2)}) collective-permute-start(bf16[8,1024]{1,0:T(8,128)(2,1)S(1)} %get-tuple-element.491), channel_id=1, source_target_pairs={{0,8},{8,16},{16,24},{1,9},{9,17},{17,25},{2,10},{10,18},{18,26},{... | collective-permute-start | bytes 49160 | tf_op jit(solution)/shard_map/while/body/eval_jaxpr/ppermute | solution.py:14
  363.3 4.3 fusion.65
  368.0 8.6 %all-reduce.5 = f32[8]{0:T(128)S(1)} all-reduce(f32[8]{0:T(128)S(1)} %get-tuple-element.477), channel_id=3, replica_groups=mesh['section'=4,'row'=2,'col'=4] {'col'}, use_global_device_ids=true, to_apply=%region_3.3.clone | all-reduce | flops 8 | bytes 64 | tf_op jit(solution)/shard_map/while
  379.0 20.5 %all-reduce.8.cloned.1.call-done = f32[8,3072]{1,0:T(8,128)} async-done(((f32[8,3072]{1,0:T(8,128)}), f32[8,3072]{1,0:T(8,128)}) %all-reduce.8.cloned.1.call-update) | async-done | bytes 98320 | tf_op jit(solution)/shard_map/while
  401.8 10.3 %all-gather.2 = bf16[4,2,2048]{2,1,0:T(2,128)(2,1)S(1)} all-gather(bf16[1,2,2048]{2,1,0:T(2,128)(2,1)S(1)} %reshape.350), channel_id=1, replica_groups=mesh['section'=4,'row'=2,'col'=4] {'col'}, dimensions={0}, use_global_device_ids=true | all-gather | bytes 40960 | tf_op jit(solution)/shard_map/while/body/eval_jaxpr/all_gather | solution.py:89
  414.9 6.3 %psum.16 = f32[8,1024]{1,0:T(8,128)S(1)} all-reduce(f32[8,1024]{1,0:T(8,128)S(1)} %fusion.77), channel_id=1, replica_groups=mesh['section'=4,'row'=2,'col'=4] {'row'}, use_global_device_ids=true, to_apply=%region_6.6 | all-reduce | flops 8192 | bytes 65536 | tf_op jit(solution)/shard_map/while/body/eval_jaxpr/psum | solution.py:93
  421.2 10.6 %collective-permute-start = (bf16[8,1024]{1,0:T(8,128)(2,1)S(1)}, bf16[8,1024]{1,0:T(8,128)(2,1)S(1)}, u32[]{:S(2)}, u32[]{:S(2)}) collective-permute-start(bf16[8,1024]{1,0:T(8,128)(2,1)S(1)} %get-tuple-element.491), channel_id=1, source_target_pairs={{0,8},{8,16},{16,24},{1,9},{9,17},{17,25},{2,10},{10,18},{18,26},{... | collective-permute-start | bytes 49160 | tf_op jit(solution)/shard_map/while/body/eval_jaxpr/ppermute | solution.py:14
  433.6 4.3 fusion.65
  438.3 8.6 %all-reduce.5 = f32[8]{0:T(128)S(1)} all-reduce(f32[8]{0:T(128)S(1)} %get-tuple-element.477), channel_id=3, replica_groups=mesh['section'=4,'row'=2,'col'=4] {'col'}, use_global_device_ids=true, to_apply=%region_3.3.clone | all-reduce | flops 8 | bytes 64 | tf_op jit(solution)/shard_map/while
  449.3 20.5 %all-reduce.8.cloned.1.call-done = f32[8,3072]{1,0:T(8,128)} async-done(((f32[8,3072]{1,0:T(8,128)}), f32[8,3072]{1,0:T(8,128)}) %all-reduce.8.cloned.1.call-update) | async-done | bytes 98320 | tf_op jit(solution)/shard_map/while
  472.1 10.3 %all-gather.2 = bf16[4,2,2048]{2,1,0:T(2,128)(2,1)S(1)} all-gather(bf16[1,2,2048]{2,1,0:T(2,128)(2,1)S(1)} %reshape.350), channel_id=1, replica_groups=mesh['section'=4,'row'=2,'col'=4] {'col'}, dimensions={0}, use_global_device_ids=true | all-gather | bytes 40960 | tf_op jit(solution)/shard_map/while/body/eval_jaxpr/all_gather | solution.py:89
  485.2 6.3 %psum.16 = f32[8,1024]{1,0:T(8,128)S(1)} all-reduce(f32[8,1024]{1,0:T(8,128)S(1)} %fusion.77), channel_id=1, replica_groups=mesh['section'=4,'row'=2,'col'=4] {'row'}, use_global_device_ids=true, to_apply=%region_6.6 | all-reduce | flops 8192 | bytes 65536 | tf_op jit(solution)/shard_map/while/body/eval_jaxpr/psum | solution.py:93
  491.6 10.6 %collective-permute-start = (bf16[8,1024]{1,0:T(8,128)(2,1)S(1)}, bf16[8,1024]{1,0:T(8,128)(2,1)S(1)}, u32[]{:S(2)}, u32[]{:S(2)}) collective-permute-start(bf16[8,1024]{1,0:T(8,128)(2,1)S(1)} %get-tuple-element.491), channel_id=1, source_target_pairs={{0,8},{8,16},{16,24},{1,9},{9,17},{17,25},{2,10},{10,18},{18,26},{... | collective-permute-start | bytes 49160 | tf_op jit(solution)/shard_map/while/body/eval_jaxpr/ppermute | solution.py:14
  (239 shorter events, 50.9 us)
Async XLA Ops:
  8.0 16.4 %copy-start.1 = (u32[32]{0:T(128)S(1)}, u32[32]{0:T(128)}, u32[]{:S(2)}) copy-start(u32[32]{0:T(128)} %get-tuple-element.547) | copy-start | bytes 388 | tf_op jit(solution)/shard_map/while
  8.0 39.9 %all-reduce.8.cloned.1.call-start = ((), (), s32[]{:S(2)}) async-start(), calls=%async_computation | async-start | bytes 196608 | tf_op jit(solution)/shard_map/while
  69.6 11.5 %collective-permute-start = (bf16[8,1024]{1,0:T(8,128)(2,1)S(1)}, bf16[8,1024]{1,0:T(8,128)(2,1)S(1)}, u32[]{:S(2)}, u32[]{:S(2)}) collective-permute-start(bf16[8,1024]{1,0:T(8,128)(2,1)S(1)} %get-tuple-element.491), channel_id=1, source_target_pairs={{0,8},{8,16},{16,24},{1,9},{9,17},{17,25},{2,10},{10,18},{18,26},{... | collective-permute-start | bytes 49160 | tf_op jit(solution)/shard_map/while/body/eval_jaxpr/ppermute | solution.py:14
  81.1 14.1 %copy-start.1 = (u32[32]{0:T(128)S(1)}, u32[32]{0:T(128)}, u32[]{:S(2)}) copy-start(u32[32]{0:T(128)} %get-tuple-element.547) | copy-start | bytes 388 | tf_op jit(solution)/shard_map/while
  81.1 37.1 %all-reduce.8.cloned.1.call-start = ((), (), s32[]{:S(2)}) async-start(), calls=%async_computation | async-start | bytes 196608 | tf_op jit(solution)/shard_map/while
  140.0 11.5 %collective-permute-start = (bf16[8,1024]{1,0:T(8,128)(2,1)S(1)}, bf16[8,1024]{1,0:T(8,128)(2,1)S(1)}, u32[]{:S(2)}, u32[]{:S(2)}) collective-permute-start(bf16[8,1024]{1,0:T(8,128)(2,1)S(1)} %get-tuple-element.491), channel_id=1, source_target_pairs={{0,8},{8,16},{16,24},{1,9},{9,17},{17,25},{2,10},{10,18},{18,26},{... | collective-permute-start | bytes 49160 | tf_op jit(solution)/shard_map/while/body/eval_jaxpr/ppermute | solution.py:14
  151.4 14.1 %copy-start.1 = (u32[32]{0:T(128)S(1)}, u32[32]{0:T(128)}, u32[]{:S(2)}) copy-start(u32[32]{0:T(128)} %get-tuple-element.547) | copy-start | bytes 388 | tf_op jit(solution)/shard_map/while
  151.4 37.1 %all-reduce.8.cloned.1.call-start = ((), (), s32[]{:S(2)}) async-start(), calls=%async_computation | async-start | bytes 196608 | tf_op jit(solution)/shard_map/while
  210.3 11.5 %collective-permute-start = (bf16[8,1024]{1,0:T(8,128)(2,1)S(1)}, bf16[8,1024]{1,0:T(8,128)(2,1)S(1)}, u32[]{:S(2)}, u32[]{:S(2)}) collective-permute-start(bf16[8,1024]{1,0:T(8,128)(2,1)S(1)} %get-tuple-element.491), channel_id=1, source_target_pairs={{0,8},{8,16},{16,24},{1,9},{9,17},{17,25},{2,10},{10,18},{18,26},{... | collective-permute-start | bytes 49160 | tf_op jit(solution)/shard_map/while/body/eval_jaxpr/ppermute | solution.py:14
  221.8 14.1 %copy-start.1 = (u32[32]{0:T(128)S(1)}, u32[32]{0:T(128)}, u32[]{:S(2)}) copy-start(u32[32]{0:T(128)} %get-tuple-element.547) | copy-start | bytes 388 | tf_op jit(solution)/shard_map/while
  221.8 37.1 %all-reduce.8.cloned.1.call-start = ((), (), s32[]{:S(2)}) async-start(), calls=%async_computation | async-start | bytes 196608 | tf_op jit(solution)/shard_map/while
  280.6 11.5 %collective-permute-start = (bf16[8,1024]{1,0:T(8,128)(2,1)S(1)}, bf16[8,1024]{1,0:T(8,128)(2,1)S(1)}, u32[]{:S(2)}, u32[]{:S(2)}) collective-permute-start(bf16[8,1024]{1,0:T(8,128)(2,1)S(1)} %get-tuple-element.491), channel_id=1, source_target_pairs={{0,8},{8,16},{16,24},{1,9},{9,17},{17,25},{2,10},{10,18},{18,26},{... | collective-permute-start | bytes 49160 | tf_op jit(solution)/shard_map/while/body/eval_jaxpr/ppermute | solution.py:14
  292.1 14.1 %copy-start.1 = (u32[32]{0:T(128)S(1)}, u32[32]{0:T(128)}, u32[]{:S(2)}) copy-start(u32[32]{0:T(128)} %get-tuple-element.547) | copy-start | bytes 388 | tf_op jit(solution)/shard_map/while
  292.1 37.1 %all-reduce.8.cloned.1.call-start = ((), (), s32[]{:S(2)}) async-start(), calls=%async_computation | async-start | bytes 196608 | tf_op jit(solution)/shard_map/while
  350.9 11.5 %collective-permute-start = (bf16[8,1024]{1,0:T(8,128)(2,1)S(1)}, bf16[8,1024]{1,0:T(8,128)(2,1)S(1)}, u32[]{:S(2)}, u32[]{:S(2)}) collective-permute-start(bf16[8,1024]{1,0:T(8,128)(2,1)S(1)} %get-tuple-element.491), channel_id=1, source_target_pairs={{0,8},{8,16},{16,24},{1,9},{9,17},{17,25},{2,10},{10,18},{18,26},{... | collective-permute-start | bytes 49160 | tf_op jit(solution)/shard_map/while/body/eval_jaxpr/ppermute | solution.py:14
  362.4 14.1 %copy-start.1 = (u32[32]{0:T(128)S(1)}, u32[32]{0:T(128)}, u32[]{:S(2)}) copy-start(u32[32]{0:T(128)} %get-tuple-element.547) | copy-start | bytes 388 | tf_op jit(solution)/shard_map/while
  362.4 37.1 %all-reduce.8.cloned.1.call-start = ((), (), s32[]{:S(2)}) async-start(), calls=%async_computation | async-start | bytes 196608 | tf_op jit(solution)/shard_map/while
  421.2 11.5 %collective-permute-start = (bf16[8,1024]{1,0:T(8,128)(2,1)S(1)}, bf16[8,1024]{1,0:T(8,128)(2,1)S(1)}, u32[]{:S(2)}, u32[]{:S(2)}) collective-permute-start(bf16[8,1024]{1,0:T(8,128)(2,1)S(1)} %get-tuple-element.491), channel_id=1, source_target_pairs={{0,8},{8,16},{16,24},{1,9},{9,17},{17,25},{2,10},{10,18},{18,26},{... | collective-permute-start | bytes 49160 | tf_op jit(solution)/shard_map/while/body/eval_jaxpr/ppermute | solution.py:14
  432.7 14.1 %copy-start.1 = (u32[32]{0:T(128)S(1)}, u32[32]{0:T(128)}, u32[]{:S(2)}) copy-start(u32[32]{0:T(128)} %get-tuple-element.547) | copy-start | bytes 388 | tf_op jit(solution)/shard_map/while
  432.7 37.1 %all-reduce.8.cloned.1.call-start = ((), (), s32[]{:S(2)}) async-start(), calls=%async_computation | async-start | bytes 196608 | tf_op jit(solution)/shard_map/while
  491.6 11.5 %collective-permute-start = (bf16[8,1024]{1,0:T(8,128)(2,1)S(1)}, bf16[8,1024]{1,0:T(8,128)(2,1)S(1)}, u32[]{:S(2)}, u32[]{:S(2)}) collective-permute-start(bf16[8,1024]{1,0:T(8,128)(2,1)S(1)} %get-tuple-element.491), channel_id=1, source_target_pairs={{0,8},{8,16},{16,24},{1,9},{9,17},{17,25},{2,10},{10,18},{18,26},{... | collective-permute-start | bytes 49160 | tf_op jit(solution)/shard_map/while/body/eval_jaxpr/ppermute | solution.py:14
  503.0 0.6 copy-start
Sparse Core Ops, SparseCore 0:
  13.5 34.4 all-reduce.7
  86.5 31.7 all-reduce.7
  156.8 31.7 all-reduce.7
  227.1 31.7 all-reduce.7
  297.4 31.7 all-reduce.7
  367.7 31.7 all-reduce.7
  438.1 31.7 all-reduce.7
where the time goes:
time: 512 us; the launch traced here: 511 us
  blocking collectives  178 us (35%)
  waiting for transfers between devices  150 us (29%)
  starting transfers between devices  74.5 us (15%)
  matrix products  55 us (11%)
  other arithmetic  19.8 us (4%)
  local copies, waits for them, and re-layouts  14.6 us (3%)
  between operations  13.4 us (3%)
    while x14, waiting for transfers between devices  144 us
    ppermute x7, starting transfers between devices, from_behind(): return lax.ppermute(x, axis, pairs)  74.4 us
    all_gather x7, blocking collectives, layer_part(): lax.all_gather(attended, 'col', axis=0, tiled=True)  71.8 us
    while x7, blocking collectives  62.2 us
    psum x7, blocking collectives, layer_part(): summed = lax.psum(mixed_rows, 'row')  44 us
    dot_general x7, matrix products, layer_part(): jnp.dot(scaled, proj_weight, preferred_element_type=jnp.float32)  30.4 us
    dot_general x7, matrix products, layer_part(): jnp.dot(lax.all_gather(attended, 'col', axis=0, tiled=True), out_weight,...  19.9 us
  transfers between devices with their start and end apart: 14, of which 14 were waited for; matrix products, arithmetic and copies ran while one was open for 3% of the time, Pallas kernels for 0%

commit v1 on v0

--- a/solution.py
+++ b/solution.py
@@ -90,7 +90,8 @@
             out_weight,
             preferred_element_type=jnp.float32,
         )
-        summed = lax.psum(mixed_rows, "row")
+        step_on_heads = lambda arr: lax.all_gather(arr, "row").sum(axis=0)
+        summed = step_on_heads(mixed_rows)
         return (h_float + summed).astype(jnp.bfloat16)
 
     def advance(tick_at, loop_state):

time: 512 us -> 492 us (0.961)
  blocking collectives: 178 us -> 158 us
  starting transfers between devices: 74.5 us -> 68.4 us
  waiting for transfers between devices: 150 us -> 156 us
    psum x7 -> x0, blocking collectives: 44 us -> none  [layer_part(): summed = lax.psum(mixed_rows, 'row')]
    all_gather x0 -> x7, blocking collectives: none -> 24 us  [layer_part(): step_on_heads = lambda arr: lax.all_gather(arr, 'row').sum(axis=0)]
    ppermute x7, starting transfers between devices: 74.4 us -> 68.3 us  [from_behind(): return lax.ppermute(x, axis, pairs)]
    while x14, waiting for transfers between devices: 144 us -> 150 us
where the time goes in v1:
time: 492 us; the launch traced here: 490 us
  blocking collectives  158 us (32%)
  waiting for transfers between devices  156 us (32%)
  starting transfers between devices  68.4 us (14%)
  matrix products  55 us (11%)
  other arithmetic  19.8 us (4%)
  local copies, waits for them, and re-layouts  14.6 us (3%)
  between operations  13.4 us (3%)
    while x14, waiting for transfers between devices  150 us
    all_gather x7, blocking collectives, layer_part(): lax.all_gather(attended, 'col', axis=0, tiled=True)  71.8 us
    ppermute x7, starting transfers between devices, from_behind(): return lax.ppermute(x, axis, pairs)  68.3 us
    while x7, blocking collectives  62.3 us
    dot_general x7, matrix products, layer_part(): jnp.dot(scaled, proj_weight, preferred_element_type=jnp.float32)  30.4 us
    all_gather x7, blocking collectives, layer_part(): step_on_heads = lambda arr: lax.all_gather(arr, 'row').sum(axis=0)  24 us
    dot_general x7, matrix products, layer_part(): jnp.dot(lax.all_gather(attended, 'col', axis=0, tiled=True), out_weight,...  19.9 us
  transfers between devices with their start and end apart: 14, of which 14 were waited for; matrix products, arithmetic and copies ran while one was open for 3% of the time, Pallas kernels for 0%

profile of v1, /device:TPU:1, one launch (start us, length us, event | category | flops | bytes accessed | tf_op | source)
XLA Modules:
  0.0 490.0 jit_solution(1584635352629555875)
XLA Ops:
  8.0 474.5 %while.18 = (s32[]{:T(128)}, bf16[8,1024]{1,0:T(8,128)(2,1)S(1)}, bf16[4,8,1024]{2,1,0:T(8,128)(2,1)S(1)}, pred[]{:T(512)}, bf16[4,8,1024]{2,1,0:T(8,128)(2,1)},...) while((s32[]{:T(128)}, bf16[8,1024]{1,0:T(8,128)(2,1)S(1)}, ...), condition=%wide.region_7.8_spmd, body=%wide.region_0.7_spmd.sunk | while | flops 86196720 | bytes 13700056 | solution.py:118
  9.0 4.3 fusion.65
  13.7 10.8 %all-reduce.5 = f32[8]{0:T(128)S(1)} all-reduce(f32[8]{0:T(128)S(1)} %get-tuple-element.477), channel_id=4, replica_groups=mesh['section'=4,'row'=2,'col'=4] {'col'}, use_global_device_ids=true, to_apply=%region_3.3.clone | all-reduce | flops 8 | bytes 64 | tf_op jit(solution)/shard_map/while
  26.9 21.0 %all-reduce.8.cloned.1.call-done = f32[8,3072]{1,0:T(8,128)} async-done(((f32[8,3072]{1,0:T(8,128)}), f32[8,3072]{1,0:T(8,128)}) %all-reduce.8.cloned.1.call-update) | async-done | bytes 98320 | tf_op jit(solution)/shard_map/while
  50.2 10.3 %all-gather.4 = bf16[4,2,2048]{2,1,0:T(2,128)(2,1)S(1)} all-gather(bf16[1,2,2048]{2,1,0:T(2,128)(2,1)S(1)} %reshape.351), channel_id=1, replica_groups=mesh['section'=4,'row'=2,'col'=4] {'col'}, dimensions={0}, use_global_device_ids=true | all-gather | bytes 40960 | tf_op jit(solution)/shard_map/while/body/eval_jaxpr/all_gather | solution.py:89
  60.5 2.8 fusion.77
  63.3 3.4 all-gather.5
  66.8 9.8 %collective-permute-start = (bf16[8,1024]{1,0:T(8,128)(2,1)S(1)}, bf16[8,1024]{1,0:T(8,128)(2,1)S(1)}, u32[]{:S(2)}, u32[]{:S(2)}) collective-permute-start(bf16[8,1024]{1,0:T(8,128)(2,1)S(1)} %get-tuple-element.491), channel_id=1, source_target_pairs={{0,8},{8,16},{16,24},{1,9},{9,17},{17,25},{2,10},{10,18},{18,26},{... | collective-permute-start | bytes 49160 | tf_op jit(solution)/shard_map/while/body/eval_jaxpr/ppermute | solution.py:14
  78.2 4.3 fusion.65
  82.9 8.6 %all-reduce.5 = f32[8]{0:T(128)S(1)} all-reduce(f32[8]{0:T(128)S(1)} %get-tuple-element.477), channel_id=4, replica_groups=mesh['section'=4,'row'=2,'col'=4] {'col'}, use_global_device_ids=true, to_apply=%region_3.3.clone | all-reduce | flops 8 | bytes 64 | tf_op jit(solution)/shard_map/while
  94.0 21.5 %all-reduce.8.cloned.1.call-done = f32[8,3072]{1,0:T(8,128)} async-done(((f32[8,3072]{1,0:T(8,128)}), f32[8,3072]{1,0:T(8,128)}) %all-reduce.8.cloned.1.call-update) | async-done | bytes 98320 | tf_op jit(solution)/shard_map/while
  117.7 10.3 %all-gather.4 = bf16[4,2,2048]{2,1,0:T(2,128)(2,1)S(1)} all-gather(bf16[1,2,2048]{2,1,0:T(2,128)(2,1)S(1)} %reshape.351), channel_id=1, replica_groups=mesh['section'=4,'row'=2,'col'=4] {'col'}, dimensions={0}, use_global_device_ids=true | all-gather | bytes 40960 | tf_op jit(solution)/shard_map/while/body/eval_jaxpr/all_gather | solution.py:89
  128.0 2.8 fusion.77
  130.8 3.4 all-gather.5
  134.3 9.8 %collective-permute-start = (bf16[8,1024]{1,0:T(8,128)(2,1)S(1)}, bf16[8,1024]{1,0:T(8,128)(2,1)S(1)}, u32[]{:S(2)}, u32[]{:S(2)}) collective-permute-start(bf16[8,1024]{1,0:T(8,128)(2,1)S(1)} %get-tuple-element.491), channel_id=1, source_target_pairs={{0,8},{8,16},{16,24},{1,9},{9,17},{17,25},{2,10},{10,18},{18,26},{... | collective-permute-start | bytes 49160 | tf_op jit(solution)/shard_map/while/body/eval_jaxpr/ppermute | solution.py:14
  145.7 4.3 fusion.65
  150.4 8.6 %all-reduce.5 = f32[8]{0:T(128)S(1)} all-reduce(f32[8]{0:T(128)S(1)} %get-tuple-element.477), channel_id=4, replica_groups=mesh['section'=4,'row'=2,'col'=4] {'col'}, use_global_device_ids=true, to_apply=%region_3.3.clone | all-reduce | flops 8 | bytes 64 | tf_op jit(solution)/shard_map/while
  161.5 21.5 %all-reduce.8.cloned.1.call-done = f32[8,3072]{1,0:T(8,128)} async-done(((f32[8,3072]{1,0:T(8,128)}), f32[8,3072]{1,0:T(8,128)}) %all-reduce.8.cloned.1.call-update) | async-done | bytes 98320 | tf_op jit(solution)/shard_map/while
  185.2 10.3 %all-gather.4 = bf16[4,2,2048]{2,1,0:T(2,128)(2,1)S(1)} all-gather(bf16[1,2,2048]{2,1,0:T(2,128)(2,1)S(1)} %reshape.351), channel_id=1, replica_groups=mesh['section'=4,'row'=2,'col'=4] {'col'}, dimensions={0}, use_global_device_ids=true | all-gather | bytes 40960 | tf_op jit(solution)/shard_map/while/body/eval_jaxpr/all_gather | solution.py:89
  195.5 2.8 fusion.77
  198.4 3.4 all-gather.5
  201.8 9.8 %collective-permute-start = (bf16[8,1024]{1,0:T(8,128)(2,1)S(1)}, bf16[8,1024]{1,0:T(8,128)(2,1)S(1)}, u32[]{:S(2)}, u32[]{:S(2)}) collective-permute-start(bf16[8,1024]{1,0:T(8,128)(2,1)S(1)} %get-tuple-element.491), channel_id=1, source_target_pairs={{0,8},{8,16},{16,24},{1,9},{9,17},{17,25},{2,10},{10,18},{18,26},{... | collective-permute-start | bytes 49160 | tf_op jit(solution)/shard_map/while/body/eval_jaxpr/ppermute | solution.py:14
  213.3 4.3 fusion.65
  218.0 8.6 %all-reduce.5 = f32[8]{0:T(128)S(1)} all-reduce(f32[8]{0:T(128)S(1)} %get-tuple-element.477), channel_id=4, replica_groups=mesh['section'=4,'row'=2,'col'=4] {'col'}, use_global_device_ids=true, to_apply=%region_3.3.clone | all-reduce | flops 8 | bytes 64 | tf_op jit(solution)/shard_map/while
  229.0 21.5 %all-reduce.8.cloned.1.call-done = f32[8,3072]{1,0:T(8,128)} async-done(((f32[8,3072]{1,0:T(8,128)}), f32[8,3072]{1,0:T(8,128)}) %all-reduce.8.cloned.1.call-update) | async-done | bytes 98320 | tf_op jit(solution)/shard_map/while
  252.8 10.3 %all-gather.4 = bf16[4,2,2048]{2,1,0:T(2,128)(2,1)S(1)} all-gather(bf16[1,2,2048]{2,1,0:T(2,128)(2,1)S(1)} %reshape.351), channel_id=1, replica_groups=mesh['section'=4,'row'=2,'col'=4] {'col'}, dimensions={0}, use_global_device_ids=true | all-gather | bytes 40960 | tf_op jit(solution)/shard_map/while/body/eval_jaxpr/all_gather | solution.py:89
  263.0 2.8 fusion.77
  265.9 3.4 all-gather.5
  269.3 9.8 %collective-permute-start = (bf16[8,1024]{1,0:T(8,128)(2,1)S(1)}, bf16[8,1024]{1,0:T(8,128)(2,1)S(1)}, u32[]{:S(2)}, u32[]{:S(2)}) collective-permute-start(bf16[8,1024]{1,0:T(8,128)(2,1)S(1)} %get-tuple-element.491), channel_id=1, source_target_pairs={{0,8},{8,16},{16,24},{1,9},{9,17},{17,25},{2,10},{10,18},{18,26},{... | collective-permute-start | bytes 49160 | tf_op jit(solution)/shard_map/while/body/eval_jaxpr/ppermute | solution.py:14
  280.8 4.3 fusion.65
  285.5 8.6 %all-reduce.5 = f32[8]{0:T(128)S(1)} all-reduce(f32[8]{0:T(128)S(1)} %get-tuple-element.477), channel_id=4, replica_groups=mesh['section'=4,'row'=2,'col'=4] {'col'}, use_global_device_ids=true, to_apply=%region_3.3.clone | all-reduce | flops 8 | bytes 64 | tf_op jit(solution)/shard_map/while
  296.5 21.5 %all-reduce.8.cloned.1.call-done = f32[8,3072]{1,0:T(8,128)} async-done(((f32[8,3072]{1,0:T(8,128)}), f32[8,3072]{1,0:T(8,128)}) %all-reduce.8.cloned.1.call-update) | async-done | bytes 98320 | tf_op jit(solution)/shard_map/while
  320.3 10.3 %all-gather.4 = bf16[4,2,2048]{2,1,0:T(2,128)(2,1)S(1)} all-gather(bf16[1,2,2048]{2,1,0:T(2,128)(2,1)S(1)} %reshape.351), channel_id=1, replica_groups=mesh['section'=4,'row'=2,'col'=4] {'col'}, dimensions={0}, use_global_device_ids=true | all-gather | bytes 40960 | tf_op jit(solution)/shard_map/while/body/eval_jaxpr/all_gather | solution.py:89
  330.6 2.8 fusion.77
  333.4 3.4 all-gather.5
  336.8 9.8 %collective-permute-start = (bf16[8,1024]{1,0:T(8,128)(2,1)S(1)}, bf16[8,1024]{1,0:T(8,128)(2,1)S(1)}, u32[]{:S(2)}, u32[]{:S(2)}) collective-permute-start(bf16[8,1024]{1,0:T(8,128)(2,1)S(1)} %get-tuple-element.491), channel_id=1, source_target_pairs={{0,8},{8,16},{16,24},{1,9},{9,17},{17,25},{2,10},{10,18},{18,26},{... | collective-permute-start | bytes 49160 | tf_op jit(solution)/shard_map/while/body/eval_jaxpr/ppermute | solution.py:14
  348.3 4.3 fusion.65
  353.0 8.6 %all-reduce.5 = f32[8]{0:T(128)S(1)} all-reduce(f32[8]{0:T(128)S(1)} %get-tuple-element.477), channel_id=4, replica_groups=mesh['section'=4,'row'=2,'col'=4] {'col'}, use_global_device_ids=true, to_apply=%region_3.3.clone | all-reduce | flops 8 | bytes 64 | tf_op jit(solution)/shard_map/while
  364.1 21.5 %all-reduce.8.cloned.1.call-done = f32[8,3072]{1,0:T(8,128)} async-done(((f32[8,3072]{1,0:T(8,128)}), f32[8,3072]{1,0:T(8,128)}) %all-reduce.8.cloned.1.call-update) | async-done | bytes 98320 | tf_op jit(solution)/shard_map/while
  387.8 10.3 %all-gather.4 = bf16[4,2,2048]{2,1,0:T(2,128)(2,1)S(1)} all-gather(bf16[1,2,2048]{2,1,0:T(2,128)(2,1)S(1)} %reshape.351), channel_id=1, replica_groups=mesh['section'=4,'row'=2,'col'=4] {'col'}, dimensions={0}, use_global_device_ids=true | all-gather | bytes 40960 | tf_op jit(solution)/shard_map/while/body/eval_jaxpr/all_gather | solution.py:89
  400.9 3.4 all-gather.5
  404.4 9.8 %collective-permute-start = (bf16[8,1024]{1,0:T(8,128)(2,1)S(1)}, bf16[8,1024]{1,0:T(8,128)(2,1)S(1)}, u32[]{:S(2)}, u32[]{:S(2)}) collective-permute-start(bf16[8,1024]{1,0:T(8,128)(2,1)S(1)} %get-tuple-element.491), channel_id=1, source_target_pairs={{0,8},{8,16},{16,24},{1,9},{9,17},{17,25},{2,10},{10,18},{18,26},{... | collective-permute-start | bytes 49160 | tf_op jit(solution)/shard_map/while/body/eval_jaxpr/ppermute | solution.py:14
  415.8 4.3 fusion.65
  420.5 8.6 %all-reduce.5 = f32[8]{0:T(128)S(1)} all-reduce(f32[8]{0:T(128)S(1)} %get-tuple-element.477), channel_id=4, replica_groups=mesh['section'=4,'row'=2,'col'=4] {'col'}, use_global_device_ids=true, to_apply=%region_3.3.clone | all-reduce | flops 8 | bytes 64 | tf_op jit(solution)/shard_map/while
  431.6 21.5 %all-reduce.8.cloned.1.call-done = f32[8,3072]{1,0:T(8,128)} async-done(((f32[8,3072]{1,0:T(8,128)}), f32[8,3072]{1,0:T(8,128)}) %all-reduce.8.cloned.1.call-update) | async-done | bytes 98320 | tf_op jit(solution)/shard_map/while
  455.3 10.3 %all-gather.4 = bf16[4,2,2048]{2,1,0:T(2,128)(2,1)S(1)} all-gather(bf16[1,2,2048]{2,1,0:T(2,128)(2,1)S(1)} %reshape.351), channel_id=1, replica_groups=mesh['section'=4,'row'=2,'col'=4] {'col'}, dimensions={0}, use_global_device_ids=true | all-gather | bytes 40960 | tf_op jit(solution)/shard_map/while/body/eval_jaxpr/all_gather | solution.py:89
  468.4 3.4 all-gather.5
  471.9 9.8 %collective-permute-start = (bf16[8,1024]{1,0:T(8,128)(2,1)S(1)}, bf16[8,1024]{1,0:T(8,128)(2,1)S(1)}, u32[]{:S(2)}, u32[]{:S(2)}) collective-permute-start(bf16[8,1024]{1,0:T(8,128)(2,1)S(1)} %get-tuple-element.491), channel_id=1, source_target_pairs={{0,8},{8,16},{16,24},{1,9},{9,17},{17,25},{2,10},{10,18},{18,26},{... | collective-permute-start | bytes 49160 | tf_op jit(solution)/shard_map/while/body/eval_jaxpr/ppermute | solution.py:14
  (246 shorter events, 50.9 us)
Async XLA Ops:
  8.0 16.4 %copy-start.1 = (u32[32]{0:T(128)S(1)}, u32[32]{0:T(128)}, u32[]{:S(2)}) copy-start(u32[32]{0:T(128)} %get-tuple-element.547) | copy-start | bytes 388 | tf_op jit(solution)/shard_map/while
  8.0 39.9 %all-reduce.8.cloned.1.call-start = ((), (), s32[]{:S(2)}) async-start(), calls=%async_computation | async-start | bytes 196608 | tf_op jit(solution)/shard_map/while
  66.8 10.6 %collective-permute-start = (bf16[8,1024]{1,0:T(8,128)(2,1)S(1)}, bf16[8,1024]{1,0:T(8,128)(2,1)S(1)}, u32[]{:S(2)}, u32[]{:S(2)}) collective-permute-start(bf16[8,1024]{1,0:T(8,128)(2,1)S(1)} %get-tuple-element.491), channel_id=1, source_target_pairs={{0,8},{8,16},{16,24},{1,9},{9,17},{17,25},{2,10},{10,18},{18,26},{... | collective-permute-start | bytes 49160 | tf_op jit(solution)/shard_map/while/body/eval_jaxpr/ppermute | solution.py:14
  77.4 14.1 %copy-start.1 = (u32[32]{0:T(128)S(1)}, u32[32]{0:T(128)}, u32[]{:S(2)}) copy-start(u32[32]{0:T(128)} %get-tuple-element.547) | copy-start | bytes 388 | tf_op jit(solution)/shard_map/while
  77.4 38.1 %all-reduce.8.cloned.1.call-start = ((), (), s32[]{:S(2)}) async-start(), calls=%async_computation | async-start | bytes 196608 | tf_op jit(solution)/shard_map/while
  134.3 10.6 %collective-permute-start = (bf16[8,1024]{1,0:T(8,128)(2,1)S(1)}, bf16[8,1024]{1,0:T(8,128)(2,1)S(1)}, u32[]{:S(2)}, u32[]{:S(2)}) collective-permute-start(bf16[8,1024]{1,0:T(8,128)(2,1)S(1)} %get-tuple-element.491), channel_id=1, source_target_pairs={{0,8},{8,16},{16,24},{1,9},{9,17},{17,25},{2,10},{10,18},{18,26},{... | collective-permute-start | bytes 49160 | tf_op jit(solution)/shard_map/while/body/eval_jaxpr/ppermute | solution.py:14
  144.9 14.1 %copy-start.1 = (u32[32]{0:T(128)S(1)}, u32[32]{0:T(128)}, u32[]{:S(2)}) copy-start(u32[32]{0:T(128)} %get-tuple-element.547) | copy-start | bytes 388 | tf_op jit(solution)/shard_map/while
  144.9 38.1 %all-reduce.8.cloned.1.call-start = ((), (), s32[]{:S(2)}) async-start(), calls=%async_computation | async-start | bytes 196608 | tf_op jit(solution)/shard_map/while
  201.8 10.6 %collective-permute-start = (bf16[8,1024]{1,0:T(8,128)(2,1)S(1)}, bf16[8,1024]{1,0:T(8,128)(2,1)S(1)}, u32[]{:S(2)}, u32[]{:S(2)}) collective-permute-start(bf16[8,1024]{1,0:T(8,128)(2,1)S(1)} %get-tuple-element.491), channel_id=1, source_target_pairs={{0,8},{8,16},{16,24},{1,9},{9,17},{17,25},{2,10},{10,18},{18,26},{... | collective-permute-start | bytes 49160 | tf_op jit(solution)/shard_map/while/body/eval_jaxpr/ppermute | solution.py:14
  212.4 14.1 %copy-start.1 = (u32[32]{0:T(128)S(1)}, u32[32]{0:T(128)}, u32[]{:S(2)}) copy-start(u32[32]{0:T(128)} %get-tuple-element.547) | copy-start | bytes 388 | tf_op jit(solution)/shard_map/while
  212.4 38.1 %all-reduce.8.cloned.1.call-start = ((), (), s32[]{:S(2)}) async-start(), calls=%async_computation | async-start | bytes 196608 | tf_op jit(solution)/shard_map/while
  269.3 10.6 %collective-permute-start = (bf16[8,1024]{1,0:T(8,128)(2,1)S(1)}, bf16[8,1024]{1,0:T(8,128)(2,1)S(1)}, u32[]{:S(2)}, u32[]{:S(2)}) collective-permute-start(bf16[8,1024]{1,0:T(8,128)(2,1)S(1)} %get-tuple-element.491), channel_id=1, source_target_pairs={{0,8},{8,16},{16,24},{1,9},{9,17},{17,25},{2,10},{10,18},{18,26},{... | collective-permute-start | bytes 49160 | tf_op jit(solution)/shard_map/while/body/eval_jaxpr/ppermute | solution.py:14
  279.9 14.1 %copy-start.1 = (u32[32]{0:T(128)S(1)}, u32[32]{0:T(128)}, u32[]{:S(2)}) copy-start(u32[32]{0:T(128)} %get-tuple-element.547) | copy-start | bytes 388 | tf_op jit(solution)/shard_map/while
  279.9 38.1 %all-reduce.8.cloned.1.call-start = ((), (), s32[]{:S(2)}) async-start(), calls=%async_computation | async-start | bytes 196608 | tf_op jit(solution)/shard_map/while
  336.8 10.6 %collective-permute-start = (bf16[8,1024]{1,0:T(8,128)(2,1)S(1)}, bf16[8,1024]{1,0:T(8,128)(2,1)S(1)}, u32[]{:S(2)}, u32[]{:S(2)}) collective-permute-start(bf16[8,1024]{1,0:T(8,128)(2,1)S(1)} %get-tuple-element.491), channel_id=1, source_target_pairs={{0,8},{8,16},{16,24},{1,9},{9,17},{17,25},{2,10},{10,18},{18,26},{... | collective-permute-start | bytes 49160 | tf_op jit(solution)/shard_map/while/body/eval_jaxpr/ppermute | solution.py:14
  347.5 14.1 %copy-start.1 = (u32[32]{0:T(128)S(1)}, u32[32]{0:T(128)}, u32[]{:S(2)}) copy-start(u32[32]{0:T(128)} %get-tuple-element.547) | copy-start | bytes 388 | tf_op jit(solution)/shard_map/while
  347.5 38.1 %all-reduce.8.cloned.1.call-start = ((), (), s32[]{:S(2)}) async-start(), calls=%async_computation | async-start | bytes 196608 | tf_op jit(solution)/shard_map/while
  404.4 10.6 %collective-permute-start = (bf16[8,1024]{1,0:T(8,128)(2,1)S(1)}, bf16[8,1024]{1,0:T(8,128)(2,1)S(1)}, u32[]{:S(2)}, u32[]{:S(2)}) collective-permute-start(bf16[8,1024]{1,0:T(8,128)(2,1)S(1)} %get-tuple-element.491), channel_id=1, source_target_pairs={{0,8},{8,16},{16,24},{1,9},{9,17},{17,25},{2,10},{10,18},{18,26},{... | collective-permute-start | bytes 49160 | tf_op jit(solution)/shard_map/while/body/eval_jaxpr/ppermute | solution.py:14
  415.0 14.1 %copy-start.1 = (u32[32]{0:T(128)S(1)}, u32[32]{0:T(128)}, u32[]{:S(2)}) copy-start(u32[32]{0:T(128)} %get-tuple-element.547) | copy-start | bytes 388 | tf_op jit(solution)/shard_map/while
  415.0 38.1 %all-reduce.8.cloned.1.call-start = ((), (), s32[]{:S(2)}) async-start(), calls=%async_computation | async-start | bytes 196608 | tf_op jit(solution)/shard_map/while
  471.9 10.6 %collective-permute-start = (bf16[8,1024]{1,0:T(8,128)(2,1)S(1)}, bf16[8,1024]{1,0:T(8,128)(2,1)S(1)}, u32[]{:S(2)}, u32[]{:S(2)}) collective-permute-start(bf16[8,1024]{1,0:T(8,128)(2,1)S(1)} %get-tuple-element.491), channel_id=1, source_target_pairs={{0,8},{8,16},{16,24},{1,9},{9,17},{17,25},{2,10},{10,18},{18,26},{... | collective-permute-start | bytes 49160 | tf_op jit(solution)/shard_map/while/body/eval_jaxpr/ppermute | solution.py:14
  482.5 0.6 copy-start
Sparse Core Ops, SparseCore 0:
  13.5 34.4 all-reduce.7
  82.7 32.6 all-reduce.7
  150.2 32.6 all-reduce.7
  217.8 32.6 all-reduce.7
  285.3 32.6 all-reduce.7
  352.8 32.6 all-reduce.7
  420.3 32.6 all-reduce.7
